TPU v7x, 128 devices: a whole 4x4x4 slice. The times are simulated.
128 devices in a mesh: ctx: 16 (over z, y), dp: 8 (over x, core).
Axes of the slice: x: 4, y: 4, z: 4, core: 2. Of those that a mesh axis runs over, the one named last changes fastest.
Arguments:
- grad_out: bfloat16 [8, 6144, 4096], P('dp', 'ctx'), may hold values from -6 to 6
- hidden: bfloat16 [8, 6144, 1792], P('dp', 'ctx'), may hold values from -6 to 6
- down_weight: bfloat16 [1792, 4096], replicated, may hold values from -0.09375 to 0.09375
Outputs:
- grad_hidden: bfloat16 [8, 6144, 1792], P('dp', 'ctx')
- weight_grad: float32 [1792, 4096], P('ctx', 'dp')
- hidden_amax: float32 [8, 1792], P('dp', 'ctx')
- grad_amax: float32 [8, 4096], P('dp', 'ctx')
All inputs are finite; a program needn't handle non-finite values.
Results may differ from a plain program's by a relative error of at most 0.006.
Values may be sent and summed in bfloat16 or wider, within the bound.
A program may use at most 192 MiB of HBM per device.

v0:
```python
import jax
import jax.numpy as jnp
from jax import lax
from jax.sharding import PartitionSpec as P

ceiling = 448.0


def from_everyone(value, axis):
    copies = jnp.broadcast_to(value, (lax.axis_size(axis), *value.shape))
    return lax.all_to_all(copies, axis, split_axis=0, concat_axis=0, tiled=True)


def over_copies(value, axis):
    everything = from_everyone(value, axis)
    return jnp.max(everything, axis=0)


def together(arrays, axis):
    line, at, outs = (jnp.concatenate([a.reshape(-1) for a in arrays]), 0, [])
    so_far = over_copies(line, axis)
    for a in arrays:
        outs.append(so_far[at : at + a.size].reshape(a.shape))
        at += a.size
    return tuple(outs)


def cut_along(value, dim, count):
    before, after = (value.shape[:dim], value.shape[dim + 1 :])
    return jnp.moveaxis(value.reshape(*before, count, -1, *after), dim, 0)


def summed_on_arrival(value, axis, dim):
    blocks = cut_along(value, dim, lax.axis_size(axis))
    arrived = lax.all_to_all(blocks, axis, split_axis=0, concat_axis=0, tiled=True)
    return arrived.sum(axis=0)


def to_grid(values, peaks):
    scaled = values.astype(jnp.float32) * (ceiling / peaks)[None, :]
    magnitude = jnp.abs(scaled)
    spacing = jnp.full_like(magnitude, 2.0 ** (-9))
    for exponent in range(-5, 9):
        spacing = jnp.where(magnitude >= 2.0**exponent, 2.0 ** (exponent - 3), spacing)
    snapped = jnp.floor(magnitude / spacing + 0.5) * spacing
    return jnp.where(scaled < 0, -snapped, snapped).astype(jnp.bfloat16)


def local_peaks(values):
    return jnp.max(jnp.abs(values.astype(jnp.float32)), axis=0)


def on_device(grad_out, hidden, down_weight):
    gdata = grad_out[0]
    hdata = hidden[0]
    ctx_count = lax.axis_size("ctx")
    position = lax.axis_index("ctx")
    ff_rows = hdata.shape[1] // ctx_count
    width_cols = gdata.shape[1] // ctx_count
    seq_total = gdata.shape[0] * ctx_count * lax.axis_size("dp")
    hpeak, gpeak = together((local_peaks(hdata), local_peaks(gdata)), "ctx")
    hpeak, gpeak = (jnp.maximum(hpeak, 1.0), jnp.maximum(gpeak, 1.0))
    result = lax.dot_general(
        gdata, down_weight, (((1,), (1,)), ((), ())), preferred_element_type=jnp.float32
    )
    grad_hidden = result.astype(jnp.bfloat16)[None]
    hquant = to_grid(hdata, hpeak)
    gquant = to_grid(gdata, gpeak)
    hscale = hpeak / ceiling
    gscale = gpeak / ceiling
    product = lax.dot_general(
        hquant, gquant, (((0,), (0,)), ((), ())), preferred_element_type=jnp.float32
    )
    partial_value = lax.psum_scatter(
        product * hscale[:, None] * gscale[None, :], "ctx", scatter_dimension=0, tiled=True
    )
    hidden_amax = lax.dynamic_slice_in_dim(hpeak, position * ff_rows, ff_rows, 0)
    summed = summed_on_arrival(partial_value, "dp", 1)
    weight_grad = summed / jnp.sqrt(jnp.float32(seq_total))
    grad_amax = lax.dynamic_slice_in_dim(gpeak, position * width_cols, width_cols, 0)
    return (grad_hidden, weight_grad, hidden_amax[None], grad_amax[None])


def solution(mesh):
    placed = (P("dp", "ctx", None), P("dp", "ctx", None), P())
    return jax.shard_map(
        on_device,
        mesh=mesh,
        in_specs=placed,
        out_specs=(P("dp", "ctx", None), P("ctx", "dp"), P("dp", "ctx"), P("dp", "ctx")),
        check_vma=False,
    )
```

profile of v0, /device:TPU:0, one launch (start us, length us, event | category | flops | bytes accessed | tf_op | source)
XLA Modules:
  0.0 269.0 jit_solution(10264941489572876904)
XLA Ops:
  7.2 0.0 copy-start
  7.2 0.0 reduce-scatter.2.cloned.1.call-start
  7.2 2.4 abs_reduce_fusion
  9.6 1.5 fusion.64
  11.1 0.2 broadcast_in_dim.109
  11.3 17.9 %all_to_all.11 = f32[16,1,5888]{2,1,0:T(1,128)S(1)} all-to-all(f32[16,1,5888]{2,1,0:T(1,128)S(1)} %broadcast_in_dim.109), channel_id=1, replica_groups=mesh['ctx'=16,'dp'=8] {'ctx'}, dimensions={0} | all-to-all | bytes 753664 | tf_op jit(solution)/shard_map/all_to_all | solution.py:11
  29.2 0.2 reduce_max.29
  29.5 0.0 copy-done
  29.5 28.1 %multiply_multiply_fusion = f32[1792,4096]{1,0:T(8,128)} fusion(f32[4096]{0:T(1024)S(1)} %get-tuple-element.6, f32[1792]{0:T(1024)S(1)} %get-tuple-element.9, bf16[1,384,4096]{2,1,0:T(8,128)(2,1)S(1)} %copy-done, f32[4096]{0:T(1024)S(1)} %get-tuple-element.5, bf16[1,384,1792]{2,1,0:T(8,128)(2,1)} %param.4, f32[1792]{0:T(1024)S(1)} %get-tuple-element.8), kind=kOutput, calls=%fused_computation | convolution fusion | flops 5740003328 | bytes 33929216 | tf_op jit(solution)/shard_map/dot_general | solution.py:71
  57.5 0.0 reduce-scatter.2.cloned.1.call-update
  57.6 172.2 %reduce-scatter.2.cloned.1.call-done = f32[112,4096]{1,0:T(8,128)} async-done(((f32[1792,4096]{1,0:T(8,128)}), f32[112,4096]{1,0:T(8,128)}) %reduce-scatter.2.cloned.1.call-update) | async-done | bytes 1835024 | tf_op jit(solution)/shard_map/reduce_scatter | solution.py:74
  229.7 3.0 %copy.16 = f32[14,8,8,512]{3,2,0,1:T(8,128)} copy(f32[14,8,8,512]{3,2,1,0:T(8,128)} %bitcast.28) | data formatting | bytes 3670016 | tf_op jit(solution)/shard_map/reshape | solution.py:30
  232.7 4.3 %all-to-all-start.1 = ((f32[8,112,512]{2,1,0:T(8,128)}), f32[8,112,512]{2,1,0:T(8,128)S(1)}, u32[]{:S(2)}, u32[]{:S(2)}) async-start(f32[8,112,512]{2,1,0:T(8,128)} %bitcast.27), calls=%async_computation.2 | async-start | bytes 3670016 | tf_op jit(solution)/shard_map/all_to_all | solution.py:35
  236.9 16.5 %fusion.66 = bf16[1,384,1792]{2,1,0:T(8,128)(2,1)} fusion(bf16[1792,4096]{1,0:T(8,128)(2,1)} %param.5, bf16[1,384,4096]{2,1,0:T(8,128)(2,1)} %param.3), kind=kOutput, calls=%fused_computation.70 | convolution fusion | flops 5637832704 | bytes 19202048 | tf_op jit(solution)/shard_map/dot_general | solution.py:63
  253.4 0.6 dynamic_slice.7
  254.0 0.6 dynamic-slice_bitcast_fusion
  254.6 6.7 %all-to-all-done.1 = f32[8,112,512]{2,1,0:T(8,128)S(1)} async-done(((f32[8,112,512]{2,1,0:T(8,128)}), f32[8,112,512]{2,1,0:T(8,128)S(1)}, u32[]{:S(2)}, u32[]{:S(2)}) %all-to-all-start.1) | async-done | bytes 1835040 | tf_op jit(solution)/shard_map/all_to_all | solution.py:35
  261.3 0.2 reduce_sum.9
  261.5 0.7 broadcast_multiply_fusion
  (3 shorter events, 0.0 us)
Async XLA Ops:
  7.2 22.3 %copy-start = (bf16[1,384,4096]{2,1,0:T(8,128)(2,1)S(1)}, bf16[1,384,4096]{2,1,0:T(8,128)(2,1)}, u32[]{:S(2)}) copy-start(bf16[1,384,4096]{2,1,0:T(8,128)(2,1)} %param.3) | copy-start | bytes 9437188
  7.2 222.6 %reduce-scatter.2.cloned.1.call-start = ((), (), s32[]{:S(2)}) async-start(), calls=%async_computation.3 | async-start | bytes 31195136 | tf_op jit(solution)/shard_map/reduce_scatter | solution.py:74
  232.7 28.6 %all-to-all-start.1 = ((f32[8,112,512]{2,1,0:T(8,128)}), f32[8,112,512]{2,1,0:T(8,128)S(1)}, u32[]{:S(2)}, u32[]{:S(2)}) async-start(f32[8,112,512]{2,1,0:T(8,128)} %bitcast.27), calls=%async_computation.2 | async-start | bytes 3670016 | tf_op jit(solution)/shard_map/all_to_all | solution.py:35
Sparse Core Ops, SparseCore 0:
  57.7 172.0 reduce-scatter.1
where the time goes:
time: 270 us; the launch traced here: 269 us
  waiting for transfers between devices  179 us (66%)
  matrix products  44.5 us (16%)
  blocking collectives  17.9 us (7%)
  between operations  14.1 us (5%)
  other arithmetic  5.03 us (2%)
  local copies, waits for them, and re-layouts  4.37 us (2%)
  starting transfers between devices  4.29 us (2%)
    reduce_scatter x1, waiting for transfers between devices, on_device(): lax.psum_scatter(product * hscale[:, None] * gscale[None, :], 'ctx', scat...  172 us
    dot_general x1, matrix products, on_device(): lax.dot_general(hquant, gquant, (((0,), (0,)), ((), ())), preferred_eleme...  28.1 us
    all_to_all x1, blocking collectives, from_everyone(): return lax.all_to_all(copies, axis, split_axis=0, concat_axis=0, tiled=True)  17.9 us
    dot_general x1, matrix products, on_device(): lax.dot_general(gdata, down_weight, (((1,), (1,)), ((), ())), preferred_e...  16.5 us
    all_to_all x1, waiting for transfers between devices, summed_on_arrival(): lax.all_to_all(blocks, axis, split_axis=0, concat_axis=0, tiled=True)  6.68 us
  transfers between devices with their start and end apart: 2, of which 2 were waited for; matrix products, arithmetic and copies ran while one was open for 7% of the time, Pallas kernels for 0%

commit v1 on v0

v1 whole, which is shorter than its diff:
```python
import functools

import jax
import jax.numpy as jnp
import numpy as np
from jax import lax
from jax.experimental import pallas as pl
from jax.experimental.pallas import tpu as pltpu
from jax.sharding import PartitionSpec as P

CEILING = 448.0
D, FFS, SEQ, REPLICAS = 4096, 1792, 6144, 8
TOK = 384
F8 = jnp.float8_e4m3fn
BF = jnp.bfloat16
F32 = jnp.float32
MESH = pl.DeviceIdType.MESH
NUDGE = np.float32((1 + 2.0**-21) * 2.0**-10)
ROWS = 112
EXTRA = ((0, 32), (32, 32), (64, 48))
PEAKS = FFS + D
GH = 256
SPLIT = 80


def kernel(g_hbm, h_hbm, w_hbm, gh_hbm, wg_ref, pk_out,
           g_own, h_own, g_peer, h_peer, w_v, gh_v, hqt, gq, hdc, gsr, acc, acce, pk,
           stage, am1, am2, am3, amy, amz, amp,
           own0, own1, own2, r10, r11, r12, r20, r21, r22, r30, r31, r32,
           lsem, wsem, osem, ssem, rsem, s2, q2):
    ctx = lax.axis_index("ctx")
    dp = lax.axis_index("dp")
    z, y, x, c = ctx // 4, ctx % 4, dp // 2, dp % 2
    own, rx1, rx2, rx3 = (own0, own1, own2), (r10, r11, r12), (r20, r21, r22), (r30, r31, r32)
    heights = (144, 144, 160)

    def dev(axis, step):
        zz, yy, xx, cc = z, y, x, c
        if axis == "z":
            zz = (z + step) % 4
        elif axis == "y":
            yy = (y + step) % 4
        elif axis == "x":
            xx = (x + step) % 4
        else:
            cc = 1 - c
        return (zz * 4 + yy, xx * 2 + cc)

    lh = pltpu.make_async_copy(h_hbm, h_own, lsem.at[0])
    lh.start()
    lg = []
    for i in range(4):
        at = pl.ds(i * 1024, 1024)
        lg.append(pltpu.make_async_copy(g_hbm.at[:, at], g_own.at[:, at], lsem.at[1 + i]))
        lg[-1].start()

    def wcopy(j):
        at = pl.ds(pl.multiple_of(j * GH, GH), GH)
        return pltpu.make_async_copy(w_hbm.at[at, :], w_v.at[at, :], wsem.at[j])

    for j in range(FFS // GH):
        wcopy(j).start()

    barrier = pltpu.get_barrier_semaphore()
    friends = [dev("y", d) for d in (1, 2, 3)] + [dev("z", d) for d in (1, 2, 3)]
    friends += [dev("x", 1), dev("x", 3), dev("c", 1)]
    for f in friends:
        pl.semaphore_signal(barrier, inc=1, device_id=f, device_id_type=MESH)

    sends = []

    def remote(src, dst, i, to, sems=None):
        a, b = sems or (ssem, rsem)
        copy = pltpu.make_async_remote_copy(
            src_ref=src, dst_ref=dst, send_sem=a.at[i], recv_sem=b.at[i],
            device_id=to, device_id_type=MESH)
        copy.start()
        sends.append(copy)
        return copy

    small = (s2, q2)

    def peak_row(ref, lo, size):
        at = pl.ds(pl.multiple_of(lo, 128), size)
        return jnp.max(jnp.abs(ref[:, at].astype(F32)), axis=0, keepdims=True)

    stage[...] = jnp.zeros_like(stage)
    lh.wait()

    def h_peaks(i, _):
        at = pl.multiple_of(i * 256, 256)
        pk[0, :, pl.ds(at, 256)] = peak_row(h_own, at, 256)
        return 0

    lax.fori_loop(0, FFS // 256, h_peaks, 0)
    pl.semaphore_wait(barrier, len(friends))
    peer = dev("c", 1)
    swaps = [remote(h_own, h_peer, 0, peer, small)]
    for i in range(4):
        lg[i].wait()
        src = pl.ds(pl.multiple_of(i * 1024 + (1 - c) * 512, 512), 512)
        swaps.append(remote(g_own.at[:, src], g_peer.at[:, pl.ds(i * 512, 512)], 1 + i, peer, small))

        def g_peaks(k, _, i=i):
            at = pl.multiple_of(i * 1024 + k * 256, 256)
            pk[0, :, pl.ds(FFS + at, 256)] = peak_row(g_own, at, 256)
            return 0

        lax.fori_loop(0, 4, g_peaks, 0)

    def spread(n):
        for r in range(16):
            size = 384 if r < 15 else 128
            yield r, slice(0, size), slice(r * 384, r * 384 + size)

    for r, a, b in spread(16):
        stage[r : r + 1, a] = pk[0, :, b]
    am1[...] = stage[...].astype(BF)
    gets = [remote(am1, amy.at[d - 1], 5 + d - 1, dev("y", d), small) for d in (1, 2, 3)]

    def gh_step(j, _):
        wcopy(j).wait()
        at = pl.ds(pl.multiple_of(j * GH, GH), GH)
        res = lax.dot_general(
            g_own[...], w_v[at, :], (((1,), (1,)), ((), ())), preferred_element_type=F32)
        gh_v[:, at] = res.astype(BF)
        return 0

    lax.fori_loop(0, 2, gh_step, 0)
    for e in gets:
        e.wait_recv()
    am2[...] = jnp.maximum(
        jnp.maximum(am1[...].astype(F32), amy[0].astype(F32)),
        jnp.maximum(amy[1].astype(F32), amy[2].astype(F32))).astype(BF)
    gets = [remote(am2, amz.at[d - 1], 8 + d - 1, dev("z", d), small) for d in (1, 2, 3)]
    lax.fori_loop(2, 4, gh_step, 0)
    for e in gets:
        e.wait_recv()
    top = jnp.maximum(
        jnp.maximum(am2[...].astype(F32), amz[0].astype(F32)),
        jnp.maximum(amz[1].astype(F32), amz[2].astype(F32)))
    am3[...] = top.astype(BF)
    swap_peaks = remote(am3, amp, 11, peer, small)

    def unpack(r, values):
        stage[...] = jnp.maximum(values, 1.0)
        for k, a, b in spread(16):
            pk[r, :, b] = stage[k : k + 1, a]

    unpack(0, top)
    pk_out[...] = pk[0]

    def on_grid(values, peaks):
        v = values.astype(F32) * ((CEILING / peaks) * 1024.0)
        return (v.astype(jnp.int32).astype(F32) * NUDGE).astype(F8)

    def quantize(r, href, gref, wide, offset):
        def h_step(i, _):
            at = pl.ds(pl.multiple_of(i * 256, 256), 256)
            peaks = pk[r, :, at]
            hqt[r, at, :] = on_grid(href[:, at], peaks).astype(BF).T
            tall = jnp.broadcast_to(peaks / CEILING, (128, 256)).T
            hdc[r, at, :] = tall
            return 0

        lax.fori_loop(0, FFS // 256, h_step, 0)

        def g_step(i, _):
            q, xr = i // 4, i % 4
            xx = (x + xr) % 4
            at = pl.ds(pl.multiple_of(xx * wide + offset + q * 128, 128), 128)
            pat = pl.ds(pl.multiple_of(FFS + xx * 1024 + c * 512 + q * 128, 128), 128)
            to = pl.ds(pl.multiple_of(xr * 128, 128), 128)
            peaks = pk[r, :, pat]
            gq[r, q, :, to] = on_grid(gref[:, at], peaks).astype(BF)
            gsr[r, q, :, to] = peaks / CEILING
            return 0

        lax.fori_loop(0, 16, g_step, 0)

    quantize(0, h_own, g_own, 1024, c * 512)
    swap_peaks.wait_recv()
    unpack(1, amp[...].astype(F32))
    for e in swaps:
        e.wait_recv()
    quantize(1, h_peer, g_peer, 512, 0)

    def gather(ref, r, offsets, size):
        return jnp.concatenate(
            [ref[r, pl.ds(pl.multiple_of(o, 16), size), :] for o in offsets], axis=0)

    def product(q, offsets, size, total):
        for r in range(2):
            left = gather(hqt, r, offsets, size)
            res = jnp.dot(left, gq[r, q], preferred_element_type=F32)
            tall = gather(hdc, r, offsets, size)
            res = res * jnp.concatenate([tall] * 4, axis=1) * gsr[r, q]
            if r == 0:
                total[...] = res
            else:
                return (res + total[...]).astype(BF)

    def task(p, k):
        if p == 1:
            base = [o * 448 + ((y + k) % 4) * ROWS for o in range(4)]
        else:
            base = [((z + k) % 4) * 448 + o * ROWS for o in range(4)]
        lo, size = EXTRA[p]
        main = product(p, base, ROWS, acc)
        more = product(3, [b + lo for b in base], size, acce.at[pl.ds(0, 4 * size)])
        for o in range(4):
            away = (o - z) % 4 if p == 1 else (o - y) % 4
            for xr in range(4):
                if p == 0:
                    to = own0.at[k, away, xr]
                elif p == 1:
                    to = own1.at[k, xr, away]
                else:
                    to = own2.at[xr, k, away]
                cols = slice(xr * 128, xr * 128 + 128)
                to[0:ROWS, :] = main[o * ROWS : (o + 1) * ROWS, cols]
                to[ROWS : ROWS + size, :] = more[o * size : (o + 1) * size, cols]

    axes = (("z", "y", "x"), ("y", "x", "z"), ("x", "z", "y"))

    def piece(ph, p, k, half):
        if ph == 0:
            return own[p].at[k, pl.ds(2 * half, 2)]
        if ph == 1:
            return own[p].at[0, k, pl.ds(2 * half, 2)]
        rows = pl.ds(0, SPLIT) if half == 0 else pl.ds(SPLIT, heights[p] - SPLIT)
        return own[p].at[0, 0, k, rows]

    def landing(ph, p, m, half):
        ref = (rx1, rx2, rx3)[ph][p].at[m]
        if ph == 2:
            return ref.at[pl.ds(0, SPLIT if half == 0 else heights[p] - SPLIT)]
        return ref

    flights = {}
    plan = {
        "a+": (0, 0, 2, 0), "c+": (0, 1, 1, 1), "b+": (0, 2, 1, 0),
        "a-": (1, 3, 2, 1), "c-": (1, 4, 3, 0), "b-": (1, 5, 3, 1),
    }

    def post(ph, p, name):
        way, m, k, half = plan[name]
        to = dev(axes[p][ph], 1 if way == 0 else 3)
        flights[ph, p, name] = remote(
            piece(ph, p, k, half), landing(ph, p, m, half), (ph * 3 + p) * 6 + m, to)

    def arrived(ph, p, name):
        flights[ph, p, name].wait_recv()
        _, m, _, half = plan[name]
        return landing(ph, p, m, half)

    def add_into(ref, others):
        total = ref[...].astype(F32)
        for o in others:
            total = total + o[...].astype(F32)
        ref[...] = total.astype(BF)

    def onward(ph, p):
        for sign, k, half in (("+", 1, 0), ("-", 3, 1)):
            got = arrived(ph, p, "a" + sign)
            mine = piece(ph, p, k, half)
            if ph == 0:
                def step(i, _, mine=mine, got=got):
                    add_into(mine.at[i // 4, i % 4], [got.at[i // 4, i % 4]])
                    return 0
                lax.fori_loop(0, 8, step, 0)
            elif ph == 1:
                for i in range(2):
                    add_into(mine.at[i], [got.at[i]])
            else:
                add_into(mine, [got])
            post(ph, p, "b" + sign)

    def gather_all(ph, p):
        refs = {n: arrived(ph, p, n) for n in ("c+", "c-", "b+", "b-")}
        return (refs["b+"], refs["c-"]), (refs["c+"], refs["b-"])

    task(0, 2)
    post(0, 0, "a+"), post(0, 0, "a-")
    task(1, 2)
    post(0, 1, "a+"), post(0, 1, "a-")

    def x_task(k, _):
        task(2, k)
        return 0

    lax.fori_loop(0, 4, x_task, 0)
    for n in ("a+", "a-", "c+", "c-"):
        post(0, 2, n)
    for p in (0, 1):
        def rest(j, _, p=p):
            task(p, (1 + 2 * j) % 5)
            return 0

        lax.fori_loop(0, 3, rest, 0)
        post(0, p, "c+"), post(0, p, "c-")

    lax.fori_loop(4, FFS // GH, gh_step, 0)
    gh_copy = pltpu.make_async_copy(gh_v, gh_hbm, osem)
    gh_copy.start()

    for p in range(3):
        onward(0, p)
    for p in range(3):
        pair = gather_all(0, p)
        for k in (2, 1, 3, 0):
            def step(i, _, k=k, pair=pair, p=p):
                add_into(own[p].at[0, k, i], [o.at[k % 2, i] for o in pair[k // 2]])
                return 0

            lax.fori_loop(0, 4, step, 0)
            if k == 2:
                post(1, p, "a+"), post(1, p, "a-")
            elif k == 1:
                post(1, p, "c+")
            elif k == 3:
                post(1, p, "c-")
    for p in range(3):
        onward(1, p)
    for p in range(3):
        pair = gather_all(1, p)
        for k in (2, 1, 3, 0):
            add_into(own[p].at[0, 0, k], [o.at[k % 2] for o in pair[k // 2]])
            if k == 2:
                post(2, p, "a+"), post(2, p, "a-")
            elif k == 1:
                post(2, p, "c+")
            elif k == 3:
                post(2, p, "c-")
    for p in range(3):
        onward(2, p)
    for p in range(3):
        pair = gather_all(2, p)
        cols = slice(p * 128, p * 128 + 128)
        lo, size = EXTRA[p]
        for half in (0, 1):
            total = piece(2, p, 0, half)[...].astype(F32)
            for o in pair[half]:
                total = total + o[...].astype(F32)
            if half == 0:
                wg_ref[0:SPLIT, cols] = total
            else:
                wg_ref[SPLIT:ROWS, cols] = total[: ROWS - SPLIT]
                wg_ref[lo : lo + size, 384:512] = total[ROWS - SPLIT :]
    for s in sends:
        s.wait_send()
    gh_copy.wait()


def on_device(grad_out, hidden, down_weight):
    vm = pltpu.VMEM
    dma = pltpu.SemaphoreType.DMA
    heights = (144, 144, 160)
    scratch = [
        vm((TOK, D), BF), vm((TOK, FFS), BF), vm((TOK, D // 2), BF), vm((TOK, FFS), BF),
        vm((FFS, D), BF), vm((TOK, FFS), BF),
        vm((2, FFS, TOK), BF), vm((2, 4, TOK, 512), BF),
        vm((2, FFS, 128), F32), vm((2, 4, 1, 512), F32),
        vm((448, 512), F32), vm((192, 512), F32), vm((2, 1, PEAKS), F32),
        vm((16, 384), F32), vm((16, 384), BF), vm((16, 384), BF), vm((16, 384), BF),
        vm((3, 16, 384), BF), vm((3, 16, 384), BF), vm((16, 384), BF),
    ]
    scratch += [vm((4, 4, 4, n, 128), BF) for n in heights]
    scratch += [vm((6, 2, 4, n, 128), BF) for n in heights]
    scratch += [vm((6, 2, n, 128), BF) for n in heights]
    scratch += [vm((6, SPLIT, 128), BF) for n in heights]
    scratch += [dma((5,)), dma((7,)), dma, dma((54,)), dma((54,)), dma((12,)), dma((12,))]
    anyspace = pl.BlockSpec(memory_space=pl.ANY)
    vmspace = pl.BlockSpec(memory_space=pltpu.VMEM)
    gh, wg, peaks = pl.pallas_call(
        kernel,
        out_shape=(
            jax.ShapeDtypeStruct((TOK, FFS), BF),
            jax.ShapeDtypeStruct((ROWS, 512), F32),
            jax.ShapeDtypeStruct((1, PEAKS), F32),
        ),
        in_specs=[anyspace] * 3,
        out_specs=(anyspace, vmspace, vmspace),
        scratch_shapes=scratch,
        compiler_params=pltpu.CompilerParams(
            collective_id=0, has_side_effects=True, vmem_limit_bytes=62 * 1024 * 1024),
    )(grad_out[0], hidden[0], down_weight)
    ctx = lax.axis_index("ctx")
    hidden_amax = lax.dynamic_slice(peaks, (0, ctx * (FFS // 16)), (1, FFS // 16))
    grad_amax = lax.dynamic_slice(peaks, (0, FFS + ctx * (D // 16)), (1, D // 16))
    return (gh[None], wg / jnp.sqrt(F32(SEQ * REPLICAS)), hidden_amax, grad_amax)


def solution(mesh):
    placed = (P("dp", "ctx", None), P("dp", "ctx", None), P())
    return jax.shard_map(
        on_device,
        mesh=mesh,
        in_specs=placed,
        out_specs=(P("dp", "ctx", None), P("ctx", "dp"), P("dp", "ctx"), P("dp", "ctx")),
        check_vma=False,
    )
```

time: 270 us -> 75.4 us (0.28)
  waiting for transfers between devices: 179 us -> 0 us
  Pallas kernels: 0 us -> 67.9 us
  matrix products: 44.5 us -> 0 us
  blocking collectives: 17.9 us -> 0 us
  between operations: 14.1 us -> 0.65 us
  starting transfers between devices: 4.29 us -> 0 us
  other arithmetic: 5.03 us -> 1.65 us
    reduce_scatter x1 -> x0, waiting for transfers between devices: 172 us -> none  [on_device(): lax.psum_scatter(product * hscale[:, None] * gscale[None, :], 'ctx', scat...]
    pallas_call x0 -> x1, Pallas kernels: none -> 67.9 us  [on_device(): pl.pallas_call(kernel, out_shape=(jax.ShapeDtypeStruct((TOK, FFS), BF), j...]
    dot_general x2 -> x0, matrix products: 44.5 us -> none  [the longest x1 28.1 us: on_device(): lax.dot_general(hquant, gquant, (((0,), (0,)), ((), ())), preferred_eleme...]
    all_to_all x1 -> x0, blocking collectives: 17.9 us -> none  [from_everyone(): return lax.all_to_all(copies, axis, split_axis=0, concat_axis=0, tiled=True)]
    all_to_all x1 -> x0, waiting for transfers between devices: 6.68 us -> none  [summed_on_arrival(): lax.all_to_all(blocks, axis, split_axis=0, concat_axis=0, tiled=True)]
    all_to_all x1 -> x0, starting transfers between devices: 4.25 us -> none  [summed_on_arrival(): lax.all_to_all(blocks, axis, split_axis=0, concat_axis=0, tiled=True)]
    reduce_max x3 -> x0, other arithmetic: 4.12 us -> none  [the longest x2 3.88 us: local_peaks(): return jnp.max(jnp.abs(values.astype(jnp.float32)), axis=0)]
    reshape x1 -> x0, local copies, waits for them, and re-layouts: 2.95 us -> none  [cut_along(): return jnp.moveaxis(value.reshape(*before, count, -1, *after), dim, 0)]
  transfers between devices with their start and end apart: 2 -> 0, of which waited for: 2 -> 0; matrix products, arithmetic and copies ran while one was open for 7% -> 0% of each run, Pallas kernels for 0% -> 0%
where the time goes in v1:
time: 75.4 us; the launch traced here: 75.2 us
  Pallas kernels  67.9 us (90%)
  local copies, waits for them, and re-layouts  4.99 us (7%)
  other arithmetic  1.65 us (2%)
    pallas_call x1, Pallas kernels, on_device(): pl.pallas_call(kernel, out_shape=(jax.ShapeDtypeStruct((TOK, FFS), BF), j...  67.9 us
    unnamed x1, local copies, waits for them, and re-layouts  2.5 us
    div x1, other arithmetic, on_device(): wg / jnp.sqrt(F32(SEQ * REPLICAS))  1.65 us

profile of v1, /device:TPU:0, one launch (start us, length us, event | category | flops | bytes accessed | tf_op | source)
XLA Modules:
  0.0 75.2 jit_solution(15123666932658428227)
XLA Ops:
  0.6 67.9 %shard_map.66 = (bf16[384,1792]{1,0:T(8,128)(2,1)}, f32[112,512]{1,0:T(8,128)}, f32[1,5888]{1,0:T(1,128)}) custom-call(bf16[384,4096]{1,0:T(8,128)(2,1)} %bitcast.3, bf16[384,1792]{1,0:T(8,128)(2,1)} %bitcast.5, bf16[1792,4096]{1,0:T(8,128)(2,1)} %w_hbm.1), custom_call_target="tpu_custom_call" | custom-call | tf_op jit(solution)/shard_map/pallas_call | solution.py:375
  68.6 1.3 %constant_dynamic-slice_fusion.1 = f32[1,112]{1,0:T(1,128)} fusion(f32[1,5888]{1,0:T(1,128)} %get-tuple-element.9, s32[]{:T(128)S(6)} %select_n.6), kind=kLoop, calls=%fused_computation.2 | loop fusion | bytes 900 | tf_op jit(solution)/shard_map/dynamic_slice | solution.py:389
  69.8 1.2 %constant_dynamic-slice_fusion = f32[1,256]{1,0:T(1,128)} fusion(f32[1,5888]{1,0:T(1,128)} %get-tuple-element.9, s32[]{:T(128)S(6)} %select_n.7), kind=kLoop, calls=%fused_computation.1 | loop fusion | bytes 2052 | tf_op jit(solution)/shard_map/dynamic_slice | solution.py:390
  71.1 1.6 %broadcast_multiply_fusion = f32[112,512]{1,0:T(8,128)} fusion(f32[112,512]{1,0:T(8,128)} %get-tuple-element.8), kind=kLoop, calls=%fused_computation | loop fusion | flops 57344 | bytes 458752 | tf_op jit(solution)/shard_map/div | solution.py:391
  72.7 2.5 %copy.8 = bf16[1,384,1792]{2,1,0:T(8,128)(2,1)} copy(bf16[1,384,1792]{2,1,0:T(8,128)(2,1)} %bitcast.4) | data formatting | bytes 2752512

commit v2 on v1

--- a/solution.py
+++ b/solution.py
@@ -11,11 +11,10 @@
 CEILING = 448.0
 D, FFS, SEQ, REPLICAS = 4096, 1792, 6144, 8
 TOK = 384
-F8 = jnp.float8_e4m3fn
 BF = jnp.bfloat16
 F32 = jnp.float32
 MESH = pl.DeviceIdType.MESH
-NUDGE = np.float32((1 + 2.0**-21) * 2.0**-10)
+NUDGE = np.float32(1 + 2.0**-21)
 ROWS = 112
 EXTRA = ((0, 32), (32, 32), (64, 48))
 PEAKS = FFS + D
@@ -24,10 +23,10 @@
 
 
 def kernel(g_hbm, h_hbm, w_hbm, gh_hbm, wg_ref, pk_out,
-           g_own, h_own, g_peer, h_peer, w_v, gh_v, hqt, gq, hdc, gsr, acc, acce, pk,
+           g_own, h_own, g_peer, w_v, gh_v, hqt, gq, pk,
            stage, am1, am2, am3, amy, amz, amp,
            own0, own1, own2, r10, r11, r12, r20, r21, r22, r30, r31, r32,
-           lsem, wsem, osem, ssem, rsem, s2, q2):
+           lsem, wsem, osem, ssem, rsem, s2, q2, hs, hr):
     ctx = lax.axis_index("ctx")
     dp = lax.axis_index("dp")
     z, y, x, c = ctx // 4, ctx % 4, dp // 2, dp % 2
@@ -58,9 +57,6 @@
         at = pl.ds(pl.multiple_of(j * GH, GH), GH)
         return pltpu.make_async_copy(w_hbm.at[at, :], w_v.at[at, :], wsem.at[j])
 
-    for j in range(FFS // GH):
-        wcopy(j).start()
-
     barrier = pltpu.get_barrier_semaphore()
     friends = [dev("y", d) for d in (1, 2, 3)] + [dev("z", d) for d in (1, 2, 3)]
     friends += [dev("x", 1), dev("x", 3), dev("c", 1)]
@@ -95,7 +91,7 @@
     lax.fori_loop(0, FFS // 256, h_peaks, 0)
     pl.semaphore_wait(barrier, len(friends))
     peer = dev("c", 1)
-    swaps = [remote(h_own, h_peer, 0, peer, small)]
+    swaps = []
     for i in range(4):
         lg[i].wait()
         src = pl.ds(pl.multiple_of(i * 1024 + (1 - c) * 512, 512), 512)
@@ -113,6 +109,8 @@
             size = 384 if r < 15 else 128
             yield r, slice(0, size), slice(r * 384, r * 384 + size)
 
+    for j in range(FFS // GH):
+        wcopy(j).start()
     for r, a, b in spread(16):
         stage[r : r + 1, a] = pk[0, :, b]
     am1[...] = stage[...].astype(BF)
@@ -152,74 +150,69 @@
 
     def on_grid(values, peaks):
         v = values.astype(F32) * ((CEILING / peaks) * 1024.0)
-        return (v.astype(jnp.int32).astype(F32) * NUDGE).astype(F8)
-
-    def quantize(r, href, gref, wide, offset):
-        def h_step(i, _):
-            at = pl.ds(pl.multiple_of(i * 256, 256), 256)
-            peaks = pk[r, :, at]
-            hqt[r, at, :] = on_grid(href[:, at], peaks).astype(BF).T
-            tall = jnp.broadcast_to(peaks / CEILING, (128, 256)).T
-            hdc[r, at, :] = tall
-            return 0
-
-        lax.fori_loop(0, FFS // 256, h_step, 0)
-
-        def g_step(i, _):
-            q, xr = i // 4, i % 4
-            xx = (x + xr) % 4
-            at = pl.ds(pl.multiple_of(xx * wide + offset + q * 128, 128), 128)
-            pat = pl.ds(pl.multiple_of(FFS + xx * 1024 + c * 512 + q * 128, 128), 128)
-            to = pl.ds(pl.multiple_of(xr * 128, 128), 128)
-            peaks = pk[r, :, pat]
-            gq[r, q, :, to] = on_grid(gref[:, at], peaks).astype(BF)
-            gsr[r, q, :, to] = peaks / CEILING
-            return 0
-
-        lax.fori_loop(0, 16, g_step, 0)
-
-    quantize(0, h_own, g_own, 1024, c * 512)
+        u = v.astype(jnp.int32).astype(F32) * NUDGE
+        big = jnp.maximum(jnp.abs(u) * 2.0**20, 1.5 * 2.0**24)
+        return (((u + big) - big) * (peaks / CEILING * 2.0**-10)).astype(BF)
+
+    def quant_g(r, q, j, lo=0, rows=TOK):
+        xx = (x + (6 - j) % 4) % 4
+        home = xx * 1024 + c * 512 + q * 128
+        at = pl.ds(pl.multiple_of(home if r == 0 else xx * 512 + q * 128, 128), 128)
+        peaks = pk[r, :, pl.ds(pl.multiple_of(FFS + home, 128), 128)]
+        ref = g_own if r == 0 else g_peer
+        to = pl.ds(pl.multiple_of(j * 128, 128), 128)
+        gq[q, pl.ds(r * TOK + lo, rows), to] = on_grid(ref[pl.ds(lo, rows), at], peaks)
+
+    hsends = []
+    for i in range(FFS // 256):
+        at = pl.ds(i * 256, 256)
+        hqt[at, 0:TOK] = on_grid(h_own[:, at], pk[0, :, at]).T
+        if i:
+            prev = pl.ds((i - 1) * 256, 256)
+            hsends.append(remote(hqt.at[prev, 0:TOK], hqt.at[prev, TOK:], i - 1, peer, (hs, hr)))
+    for j in range(2):
+        for q in (2, 3):
+            quant_g(0, q, j)
+        if j == 0:
+            prev = pl.ds(FFS - 256, 256)
+            hsends.append(remote(hqt.at[prev, 0:TOK], hqt.at[prev, TOK:], 6, peer, (hs, hr)))
     swap_peaks.wait_recv()
     unpack(1, amp[...].astype(F32))
     for e in swaps:
         e.wait_recv()
-    quantize(1, h_peer, g_peer, 512, 0)
-
-    def gather(ref, r, offsets, size):
-        return jnp.concatenate(
-            [ref[r, pl.ds(pl.multiple_of(o, 16), size), :] for o in offsets], axis=0)
-
-    def product(q, offsets, size, total):
-        for r in range(2):
-            left = gather(hqt, r, offsets, size)
-            res = jnp.dot(left, gq[r, q], preferred_element_type=F32)
-            tall = gather(hdc, r, offsets, size)
-            res = res * jnp.concatenate([tall] * 4, axis=1) * gsr[r, q]
-            if r == 0:
-                total[...] = res
-            else:
-                return (res + total[...]).astype(BF)
-
-    def task(p, k):
+    for j in range(2):
+        for q in (2, 3):
+            quant_g(1, q, j)
+    for e in hsends:
+        e.wait_recv()
+
+    def product(q, offsets, size, cols):
+        left = jnp.concatenate(
+            [hqt[pl.ds(pl.multiple_of(o, 16), size), :] for o in offsets], axis=0)
+        return jnp.dot(left, gq[q, :, cols], preferred_element_type=F32).astype(BF)
+
+    def blocks(p, k, j0, count):
         if p == 1:
             base = [o * 448 + ((y + k) % 4) * ROWS for o in range(4)]
         else:
             base = [((z + k) % 4) * 448 + o * ROWS for o in range(4)]
         lo, size = EXTRA[p]
-        main = product(p, base, ROWS, acc)
-        more = product(3, [b + lo for b in base], size, acce.at[pl.ds(0, 4 * size)])
+        cols = slice(j0 * 128, (j0 + count) * 128)
+        main = product(p, base, ROWS, cols)
+        more = product(3, [b + lo for b in base], size, cols)
         for o in range(4):
             away = (o - z) % 4 if p == 1 else (o - y) % 4
-            for xr in range(4):
+            for j in range(count):
+                xr = (6 - j0 - j) % 4
                 if p == 0:
                     to = own0.at[k, away, xr]
                 elif p == 1:
                     to = own1.at[k, xr, away]
                 else:
                     to = own2.at[xr, k, away]
-                cols = slice(xr * 128, xr * 128 + 128)
-                to[0:ROWS, :] = main[o * ROWS : (o + 1) * ROWS, cols]
-                to[ROWS : ROWS + size, :] = more[o * size : (o + 1) * size, cols]
+                at = slice(j * 128, j * 128 + 128)
+                to[0:ROWS, :] = main[o * ROWS : (o + 1) * ROWS, at]
+                to[ROWS : ROWS + size, :] = more[o * size : (o + 1) * size, at]
 
     axes = (("z", "y", "x"), ("y", "x", "z"), ("x", "z", "y"))
 
@@ -280,21 +273,34 @@
         refs = {n: arrived(ph, p, n) for n in ("c+", "c-", "b+", "b-")}
         return (refs["b+"], refs["c-"]), (refs["c+"], refs["b-"])
 
-    task(0, 2)
+    def x_first(k, _):
+        blocks(2, k, 0, 2)
+        for r in range(2):
+            quant_g(r, 0, k)
+            quant_g(r, 3, 2 + k // 2, pl.multiple_of((k % 2) * (TOK // 2), TOK // 2), TOK // 2)
+        return 0
+
+    lax.fori_loop(0, 4, x_first, 0)
+    for n in ("a+", "a-", "c+"):
+        post(0, 2, n)
+    blocks(0, 2, 0, 4)
+    for j in range(4):
+        quant_g(0, 1, j), quant_g(1, 1, j)
     post(0, 0, "a+"), post(0, 0, "a-")
-    task(1, 2)
+    blocks(1, 2, 0, 4)
+    for j in (2, 3):
+        quant_g(0, 2, j), quant_g(1, 2, j)
     post(0, 1, "a+"), post(0, 1, "a-")
 
-    def x_task(k, _):
-        task(2, k)
+    def x_second(k, _):
+        blocks(2, k, 2, 2)
         return 0
 
-    lax.fori_loop(0, 4, x_task, 0)
-    for n in ("a+", "a-", "c+", "c-"):
-        post(0, 2, n)
+    lax.fori_loop(0, 4, x_second, 0)
+    post(0, 2, "c-")
     for p in (0, 1):
         def rest(j, _, p=p):
-            task(p, (1 + 2 * j) % 5)
+            blocks(p, (1 + 2 * j) % 5, 0, 4)
             return 0
 
         lax.fori_loop(0, 3, rest, 0)
@@ -304,9 +310,9 @@
     gh_copy = pltpu.make_async_copy(gh_v, gh_hbm, osem)
     gh_copy.start()
 
-    for p in range(3):
+    for p in (2, 0, 1):
         onward(0, p)
-    for p in range(3):
+    for p in (2, 0, 1):
         pair = gather_all(0, p)
         for k in (2, 1, 3, 0):
             def step(i, _, k=k, pair=pair, p=p):
@@ -320,9 +326,9 @@
                 post(1, p, "c+")
             elif k == 3:
                 post(1, p, "c-")
-    for p in range(3):
+    for p in (2, 0, 1):
         onward(1, p)
-    for p in range(3):
+    for p in (2, 0, 1):
         pair = gather_all(1, p)
         for k in (2, 1, 3, 0):
             add_into(own[p].at[0, 0, k], [o.at[k % 2] for o in pair[k // 2]])
@@ -332,9 +338,9 @@
                 post(2, p, "c+")
             elif k == 3:
                 post(2, p, "c-")
-    for p in range(3):
+    for p in (2, 0, 1):
         onward(2, p)
-    for p in range(3):
+    for p in (2, 0, 1):
         pair = gather_all(2, p)
         cols = slice(p * 128, p * 128 + 128)
         lo, size = EXTRA[p]
@@ -352,16 +358,35 @@
     gh_copy.wait()
 
 
+def finish(gh_hbm, wg, pk, gh_out, wg_out, ha_out, ga_out, buf, isem, osem):
+    step = TOK // 4
+    rows = [pl.ds(i * step, step) for i in range(4)]
+    ins = [pltpu.make_async_copy(gh_hbm.at[r], buf.at[r], isem.at[i]) for i, r in enumerate(rows)]
+    outs = [pltpu.make_async_copy(buf.at[r], gh_out.at[r], osem.at[i]) for i, r in enumerate(rows)]
+    for e in ins:
+        e.start()
+    wg_out[...] = wg[...] * np.float32(1.0 / np.sqrt(SEQ * REPLICAS))
+    ctx = lax.axis_index("ctx")
+    some = pk[:, 0:ROWS]
+    for k in range(1, 16):
+        some = jnp.where(ctx == k, pk[:, k * ROWS : (k + 1) * ROWS], some)
+    ha_out[...] = some
+    ga_out[...] = pk[:, pl.ds(pl.multiple_of(FFS + ctx * 256, 256), 256)]
+    for a, b in zip(ins, outs):
+        a.wait()
+        b.start()
+    for b in outs:
+        b.wait()
+
+
 def on_device(grad_out, hidden, down_weight):
     vm = pltpu.VMEM
     dma = pltpu.SemaphoreType.DMA
     heights = (144, 144, 160)
     scratch = [
-        vm((TOK, D), BF), vm((TOK, FFS), BF), vm((TOK, D // 2), BF), vm((TOK, FFS), BF),
+        vm((TOK, D), BF), vm((TOK, FFS), BF), vm((TOK, D // 2), BF),
         vm((FFS, D), BF), vm((TOK, FFS), BF),
-        vm((2, FFS, TOK), BF), vm((2, 4, TOK, 512), BF),
-        vm((2, FFS, 128), F32), vm((2, 4, 1, 512), F32),
-        vm((448, 512), F32), vm((192, 512), F32), vm((2, 1, PEAKS), F32),
+        vm((FFS, 2 * TOK), BF), vm((4, 2 * TOK, 512), BF), vm((2, 1, PEAKS), F32),
         vm((16, 384), F32), vm((16, 384), BF), vm((16, 384), BF), vm((16, 384), BF),
         vm((3, 16, 384), BF), vm((3, 16, 384), BF), vm((16, 384), BF),
     ]
@@ -369,7 +394,7 @@
     scratch += [vm((6, 2, 4, n, 128), BF) for n in heights]
     scratch += [vm((6, 2, n, 128), BF) for n in heights]
     scratch += [vm((6, SPLIT, 128), BF) for n in heights]
-    scratch += [dma((5,)), dma((7,)), dma, dma((54,)), dma((54,)), dma((12,)), dma((12,))]
+    scratch += [dma((5,)), dma((7,)), dma, dma((54,)), dma((54,)), dma((12,)), dma((12,)), dma((7,)), dma((7,))]
     anyspace = pl.BlockSpec(memory_space=pl.ANY)
     vmspace = pl.BlockSpec(memory_space=pltpu.VMEM)
     gh, wg, peaks = pl.pallas_call(
@@ -385,10 +410,19 @@
         compiler_params=pltpu.CompilerParams(
             collective_id=0, has_side_effects=True, vmem_limit_bytes=62 * 1024 * 1024),
     )(grad_out[0], hidden[0], down_weight)
-    ctx = lax.axis_index("ctx")
-    hidden_amax = lax.dynamic_slice(peaks, (0, ctx * (FFS // 16)), (1, FFS // 16))
-    grad_amax = lax.dynamic_slice(peaks, (0, FFS + ctx * (D // 16)), (1, D // 16))
-    return (gh[None], wg / jnp.sqrt(F32(SEQ * REPLICAS)), hidden_amax, grad_amax)
+    gh, wg, ha, ga = pl.pallas_call(
+        finish,
+        out_shape=(
+            jax.ShapeDtypeStruct((TOK, FFS), BF),
+            jax.ShapeDtypeStruct((ROWS, 512), F32),
+            jax.ShapeDtypeStruct((1, ROWS), F32),
+            jax.ShapeDtypeStruct((1, 256), F32),
+        ),
+        in_specs=[anyspace, vmspace, vmspace],
+        out_specs=(anyspace, vmspace, vmspace, vmspace),
+        scratch_shapes=[vm((TOK, FFS), BF), dma((4,)), dma((4,))],
+    )(gh, wg, peaks)
+    return (gh[None], wg, ha, ga)
 
 
 def solution(mesh):

time: 75.4 us -> 65.9 us (0.87)
  local copies, waits for them, and re-layouts: 4.99 us -> 0 us
  Pallas kernels: 67.9 us -> 65.1 us
  other arithmetic: 1.65 us -> 0 us
    pallas_call x1, Pallas kernels: 67.9 us -> 61.2 us  [on_device(): pl.pallas_call(kernel, out_shape=(jax.ShapeDtypeStruct((TOK, FFS), BF), j...]
    pallas_call x0 -> x1, Pallas kernels: none -> 3.91 us  [on_device(): pl.pallas_call(finish, out_shape=(jax.ShapeDtypeStruct((TOK, FFS), BF), j...]
    unnamed x1 -> x0, local copies, waits for them, and re-layouts: 2.5 us -> none
    dynamic_slice x2 -> x0, local copies, waits for them, and re-layouts: 2.48 us -> none  [the longest x1 1.26 us: on_device(): lax.dynamic_slice(peaks, (0, ctx * (FFS // 16)), (1, FFS // 16))]
    div x1 -> x0, other arithmetic: 1.65 us -> none  [on_device(): wg / jnp.sqrt(F32(SEQ * REPLICAS))]
where the time goes in v2:
time: 65.9 us; the launch traced here: 65.7 us
  Pallas kernels  65.1 us (99%)
    pallas_call x1, Pallas kernels, on_device(): pl.pallas_call(kernel, out_shape=(jax.ShapeDtypeStruct((TOK, FFS), BF), j...  61.2 us
    pallas_call x1, Pallas kernels, on_device(): pl.pallas_call(finish, out_shape=(jax.ShapeDtypeStruct((TOK, FFS), BF), j...  3.91 us

profile of v2, /device:TPU:0, one launch (start us, length us, event | category | flops | bytes accessed | tf_op | source)
XLA Modules:
  0.0 65.7 jit_solution(5691763697643958850)
XLA Ops:
  0.6 61.2 %shard_map.66 = (bf16[384,1792]{1,0:T(8,128)(2,1)}, f32[112,512]{1,0:T(8,128)}, f32[1,5888]{1,0:T(1,128)}) custom-call(bf16[384,4096]{1,0:T(8,128)(2,1)} %bitcast.3, bf16[384,1792]{1,0:T(8,128)(2,1)} %bitcast.4, bf16[1792,4096]{1,0:T(8,128)(2,1)} %w_hbm.1), custom_call_target="tpu_custom_call" | custom-call | tf_op jit(solution)/shard_map/pallas_call | solution.py:400
  61.8 3.9 %shard_map.67 = (bf16[384,1792]{1,0:T(8,128)(2,1)}, f32[112,512]{1,0:T(8,128)}, f32[1,112]{1,0:T(1,128)}, f32[1,256]{1,0:T(1,128)}) custom-call(bf16[384,1792]{1,0:T(8,128)(2,1)} %get-tuple-element.11.gh_hbm, f32[112,512]{1,0:T(8,128)} %get-tuple-element.12.wg, f32[1,5888]{1,0:T(1,128)} %get-tuple-element.13.pk), custom_call_target="tpu_custom_call" | custom-call | tf_op jit(solution)/shard_map/pallas_call | solution.py:413

commit v3 on v2

--- a/solution.py
+++ b/solution.py
@@ -22,11 +22,11 @@
 SPLIT = 80
 
 
-def kernel(g_hbm, h_hbm, w_hbm, gh_hbm, wg_ref, pk_out,
-           g_own, h_own, g_peer, w_v, gh_v, hqt, gq, pk,
+def kernel(g_hbm, h_hbm, w_hbm, gh_v, wg_ref, pk_out,
+           g_own, h_own, g_peer, w_v, hqt, gq, pk,
            stage, am1, am2, am3, amy, amz, amp,
            own0, own1, own2, r10, r11, r12, r20, r21, r22, r30, r31, r32,
-           lsem, wsem, osem, ssem, rsem, s2, q2, hs, hr):
+           lsem, wsem, ssem, rsem, s2, q2, hs, hr):
     ctx = lax.axis_index("ctx")
     dp = lax.axis_index("dp")
     z, y, x, c = ctx // 4, ctx % 4, dp // 2, dp % 2
@@ -114,7 +114,7 @@
     for r, a, b in spread(16):
         stage[r : r + 1, a] = pk[0, :, b]
     am1[...] = stage[...].astype(BF)
-    gets = [remote(am1, amy.at[d - 1], 5 + d - 1, dev("y", d), small) for d in (1, 2, 3)]
+    gets = [remote(am1, amy.at[d - 1], 5 + d - 1, dev("y", d), small) for d in (2, 1, 3)]
 
     def gh_step(j, _):
         wcopy(j).wait()
@@ -124,14 +124,14 @@
         gh_v[:, at] = res.astype(BF)
         return 0
 
-    lax.fori_loop(0, 2, gh_step, 0)
+    gh_step(0, 0)
     for e in gets:
         e.wait_recv()
     am2[...] = jnp.maximum(
         jnp.maximum(am1[...].astype(F32), amy[0].astype(F32)),
         jnp.maximum(amy[1].astype(F32), amy[2].astype(F32))).astype(BF)
-    gets = [remote(am2, amz.at[d - 1], 8 + d - 1, dev("z", d), small) for d in (1, 2, 3)]
-    lax.fori_loop(2, 4, gh_step, 0)
+    gets = [remote(am2, amz.at[d - 1], 8 + d - 1, dev("z", d), small) for d in (2, 1, 3)]
+    lax.fori_loop(1, 3, gh_step, 0)
     for e in gets:
         e.wait_recv()
     top = jnp.maximum(
@@ -176,6 +176,11 @@
         if j == 0:
             prev = pl.ds(FFS - 256, 256)
             hsends.append(remote(hqt.at[prev, 0:TOK], hqt.at[prev, TOK:], 6, peer, (hs, hr)))
+    for j in range(4):
+        quant_g(0, 0, j)
+        quant_g(0, 1, j)
+        if j > 1:
+            quant_g(0, 2, j), quant_g(0, 3, j)
     swap_peaks.wait_recv()
     unpack(1, amp[...].astype(F32))
     for e in swaps:
@@ -183,6 +188,10 @@
     for j in range(2):
         for q in (2, 3):
             quant_g(1, q, j)
+    for j in range(4):
+        quant_g(1, 0, j)
+        if j > 1:
+            quant_g(1, 3, j)
     for e in hsends:
         e.wait_recv()
 
@@ -240,12 +249,22 @@
         way, m, k, half = plan[name]
         to = dev(axes[p][ph], 1 if way == 0 else 3)
         flights[ph, p, name] = remote(
-            piece(ph, p, k, half), landing(ph, p, m, half), (ph * 3 + p) * 6 + m, to)
-
-    def arrived(ph, p, name):
-        flights[ph, p, name].wait_recv()
+            piece(ph, p, k, half), landing(ph, p, m, half), (ph * 3 + p) * 8 + m, to)
+
+    def post_part(ph, p, name, idx):
+        way, m, k, half = plan[name]
+        to = dev(axes[p][ph], 1 if way == 0 else 3)
+        sem = (ph * 3 + p) * 8 + (m if idx == 0 else 6 + way)
+        flights[ph, p, name, idx] = remote(
+            piece(ph, p, k, half).at[idx], landing(ph, p, m, half).at[idx], sem, to)
+
+    def arrived(ph, p, name, idx=None):
+        key = (ph, p, name) if idx is None else (ph, p, name, idx)
+        if key in flights:
+            flights.pop(key).wait_recv()
         _, m, _, half = plan[name]
-        return landing(ph, p, m, half)
+        ref = landing(ph, p, m, half)
+        return ref if idx is None else ref.at[idx]
 
     def add_into(ref, others):
         total = ref[...].astype(F32)
@@ -253,91 +272,78 @@
             total = total + o[...].astype(F32)
         ref[...] = total.astype(BF)
 
+    def add_rows(ph, ref, others):
+        if ph:
+            add_into(ref, others)
+            return
+
+        def step(i, _):
+            add_into(ref.at[i], [o.at[i] for o in others])
+            return 0
+
+        lax.fori_loop(0, 4, step, 0)
+
     def onward(ph, p):
-        for sign, k, half in (("+", 1, 0), ("-", 3, 1)):
+        order = (("-", 0), ("+", 1), ("-", 1), ("+", 0))
+        for sign, idx in order if ph < 2 else (("+", None), ("-", None)):
             got = arrived(ph, p, "a" + sign)
+            _, _, k, half = plan["b" + sign]
             mine = piece(ph, p, k, half)
-            if ph == 0:
-                def step(i, _, mine=mine, got=got):
-                    add_into(mine.at[i // 4, i % 4], [got.at[i // 4, i % 4]])
-                    return 0
-                lax.fori_loop(0, 8, step, 0)
-            elif ph == 1:
-                for i in range(2):
-                    add_into(mine.at[i], [got.at[i]])
+            if ph < 2:
+                add_rows(ph, mine.at[idx], [got.at[idx]])
+                post_part(ph, p, "b" + sign, idx)
             else:
                 add_into(mine, [got])
-            post(ph, p, "b" + sign)
+                post(ph, p, "b" + sign)
+
+    def settle(ph):
+        for k in (2, 1, 3, 0):
+            for p in (2, 0, 1):
+                idx = k % 2
+                if k < 2:
+                    refs = [arrived(ph, p, "c-").at[idx], arrived(ph, p, "b+", idx)]
+                else:
+                    refs = [arrived(ph, p, "c+").at[idx], arrived(ph, p, "b-", idx)]
+                add_rows(ph, own[p].at[(0,) * (ph + 1) + (k,)], refs)
+                if k == 2:
+                    post(ph + 1, p, "a+"), post(ph + 1, p, "a-")
+                elif k:
+                    post(ph + 1, p, "c+" if k == 1 else "c-")
 
     def gather_all(ph, p):
         refs = {n: arrived(ph, p, n) for n in ("c+", "c-", "b+", "b-")}
         return (refs["b+"], refs["c-"]), (refs["c+"], refs["b-"])
 
-    def x_first(k, _):
+    for k in range(4):
         blocks(2, k, 0, 2)
-        for r in range(2):
-            quant_g(r, 0, k)
-            quant_g(r, 3, 2 + k // 2, pl.multiple_of((k % 2) * (TOK // 2), TOK // 2), TOK // 2)
-        return 0
-
-    lax.fori_loop(0, 4, x_first, 0)
     for n in ("a+", "a-", "c+"):
         post(0, 2, n)
     blocks(0, 2, 0, 4)
     for j in range(4):
-        quant_g(0, 1, j), quant_g(1, 1, j)
+        quant_g(1, 1, j)
     post(0, 0, "a+"), post(0, 0, "a-")
     blocks(1, 2, 0, 4)
     for j in (2, 3):
-        quant_g(0, 2, j), quant_g(1, 2, j)
+        quant_g(1, 2, j)
     post(0, 1, "a+"), post(0, 1, "a-")
-
-    def x_second(k, _):
+    for k in range(4):
         blocks(2, k, 2, 2)
-        return 0
-
-    lax.fori_loop(0, 4, x_second, 0)
     post(0, 2, "c-")
     for p in (0, 1):
-        def rest(j, _, p=p):
-            blocks(p, (1 + 2 * j) % 5, 0, 4)
-            return 0
-
-        lax.fori_loop(0, 3, rest, 0)
-        post(0, p, "c+"), post(0, p, "c-")
-
-    lax.fori_loop(4, FFS // GH, gh_step, 0)
-    gh_copy = pltpu.make_async_copy(gh_v, gh_hbm, osem)
-    gh_copy.start()
+        for k in (1, 3):
+            blocks(p, k, 0, 4)
+            post(0, p, "c+" if k == 1 else "c-")
+    for p in (0, 1):
+        blocks(p, 0, 0, 4)
+
+    lax.fori_loop(3, FFS // GH, gh_step, 0)
 
     for p in (2, 0, 1):
         onward(0, p)
-    for p in (2, 0, 1):
-        pair = gather_all(0, p)
-        for k in (2, 1, 3, 0):
-            def step(i, _, k=k, pair=pair, p=p):
-                add_into(own[p].at[0, k, i], [o.at[k % 2, i] for o in pair[k // 2]])
-                return 0
-
-            lax.fori_loop(0, 4, step, 0)
-            if k == 2:
-                post(1, p, "a+"), post(1, p, "a-")
-            elif k == 1:
-                post(1, p, "c+")
-            elif k == 3:
-                post(1, p, "c-")
+    settle(0)
     for p in (2, 0, 1):
         onward(1, p)
-    for p in (2, 0, 1):
-        pair = gather_all(1, p)
-        for k in (2, 1, 3, 0):
-            add_into(own[p].at[0, 0, k], [o.at[k % 2] for o in pair[k // 2]])
-            if k == 2:
-                post(2, p, "a+"), post(2, p, "a-")
-            elif k == 1:
-                post(2, p, "c+")
-            elif k == 3:
-                post(2, p, "c-")
+    settle(1)
     for p in (2, 0, 1):
         onward(2, p)
     for p in (2, 0, 1):
@@ -355,16 +361,11 @@
                 wg_ref[lo : lo + size, 384:512] = total[ROWS - SPLIT :]
     for s in sends:
         s.wait_send()
-    gh_copy.wait()
-
-
-def finish(gh_hbm, wg, pk, gh_out, wg_out, ha_out, ga_out, buf, isem, osem):
-    step = TOK // 4
-    rows = [pl.ds(i * step, step) for i in range(4)]
-    ins = [pltpu.make_async_copy(gh_hbm.at[r], buf.at[r], isem.at[i]) for i, r in enumerate(rows)]
-    outs = [pltpu.make_async_copy(buf.at[r], gh_out.at[r], osem.at[i]) for i, r in enumerate(rows)]
-    for e in ins:
-        e.start()
+
+
+def finish(gh, wg, pk, gh_out, wg_out, ha_out, ga_out, osem):
+    out = pltpu.make_async_copy(gh, gh_out, osem)
+    out.start()
     wg_out[...] = wg[...] * np.float32(1.0 / np.sqrt(SEQ * REPLICAS))
     ctx = lax.axis_index("ctx")
     some = pk[:, 0:ROWS]
@@ -372,11 +373,7 @@
         some = jnp.where(ctx == k, pk[:, k * ROWS : (k + 1) * ROWS], some)
     ha_out[...] = some
     ga_out[...] = pk[:, pl.ds(pl.multiple_of(FFS + ctx * 256, 256), 256)]
-    for a, b in zip(ins, outs):
-        a.wait()
-        b.start()
-    for b in outs:
-        b.wait()
+    out.wait()
 
 
 def on_device(grad_out, hidden, down_weight):
@@ -385,7 +382,7 @@
     heights = (144, 144, 160)
     scratch = [
         vm((TOK, D), BF), vm((TOK, FFS), BF), vm((TOK, D // 2), BF),
-        vm((FFS, D), BF), vm((TOK, FFS), BF),
+        vm((FFS, D), BF),
         vm((FFS, 2 * TOK), BF), vm((4, 2 * TOK, 512), BF), vm((2, 1, PEAKS), F32),
         vm((16, 384), F32), vm((16, 384), BF), vm((16, 384), BF), vm((16, 384), BF),
         vm((3, 16, 384), BF), vm((3, 16, 384), BF), vm((16, 384), BF),
@@ -394,8 +391,8 @@
     scratch += [vm((6, 2, 4, n, 128), BF) for n in heights]
     scratch += [vm((6, 2, n, 128), BF) for n in heights]
     scratch += [vm((6, SPLIT, 128), BF) for n in heights]
-    scratch += [dma((5,)), dma((7,)), dma, dma((54,)), dma((54,)), dma((12,)), dma((12,)), dma((7,)), dma((7,))]
-    anyspace = pl.BlockSpec(memory_space=pl.ANY)
+    scratch += [dma((5,)), dma((7,)), dma((72,)), dma((72,)), dma((12,)), dma((12,)), dma((7,)), dma((7,))]
+    hbm = pl.BlockSpec(memory_space=pltpu.HBM)
     vmspace = pl.BlockSpec(memory_space=pltpu.VMEM)
     gh, wg, peaks = pl.pallas_call(
         kernel,
@@ -404,11 +401,11 @@
             jax.ShapeDtypeStruct((ROWS, 512), F32),
             jax.ShapeDtypeStruct((1, PEAKS), F32),
         ),
-        in_specs=[anyspace] * 3,
-        out_specs=(anyspace, vmspace, vmspace),
+        in_specs=[hbm] * 3,
+        out_specs=(vmspace, vmspace, vmspace),
         scratch_shapes=scratch,
         compiler_params=pltpu.CompilerParams(
-            collective_id=0, has_side_effects=True, vmem_limit_bytes=62 * 1024 * 1024),
+            collective_id=0, has_side_effects=True, vmem_limit_bytes=54_000_000),
     )(grad_out[0], hidden[0], down_weight)
     gh, wg, ha, ga = pl.pallas_call(
         finish,
@@ -418,9 +415,10 @@
             jax.ShapeDtypeStruct((1, ROWS), F32),
             jax.ShapeDtypeStruct((1, 256), F32),
         ),
-        in_specs=[anyspace, vmspace, vmspace],
-        out_specs=(anyspace, vmspace, vmspace, vmspace),
-        scratch_shapes=[vm((TOK, FFS), BF), dma((4,)), dma((4,))],
+        in_specs=[vmspace, vmspace, vmspace],
+        out_specs=(hbm, vmspace, vmspace, vmspace),
+        scratch_shapes=[dma],
+        compiler_params=pltpu.CompilerParams(vmem_limit_bytes=8 * 1024 * 1024),
     )(gh, wg, peaks)
     return (gh[None], wg, ha, ga)
 

time: 65.9 us -> 59.7 us (0.906)
  Pallas kernels: 65.1 us -> 59 us
    pallas_call x1, Pallas kernels: 61.2 us -> 57.1 us  [on_device(): pl.pallas_call(kernel, out_shape=(jax.ShapeDtypeStruct((TOK, FFS), BF), j...]
    pallas_call x1, Pallas kernels: 3.91 us -> 1.82 us  [on_device(): pl.pallas_call(finish, out_shape=(jax.ShapeDtypeStruct((TOK, FFS), BF), j...]
where the time goes in v3:
time: 59.7 us; the launch traced here: 59.6 us
  Pallas kernels  59 us (99%)
  between operations  0.64 us (1%)
    pallas_call x1, Pallas kernels, on_device(): pl.pallas_call(kernel, out_shape=(jax.ShapeDtypeStruct((TOK, FFS), BF), j...  57.1 us
    pallas_call x1, Pallas kernels, on_device(): pl.pallas_call(finish, out_shape=(jax.ShapeDtypeStruct((TOK, FFS), BF), j...  1.82 us

profile of v3, /device:TPU:0, one launch (start us, length us, event | category | flops | bytes accessed | tf_op | source)
XLA Modules:
  0.0 59.6 jit_solution(5143237505862343406)
XLA Ops:
  0.6 57.1 %shard_map.66 = (bf16[384,1792]{1,0:T(8,128)(2,1)S(1)}, f32[112,512]{1,0:T(8,128)S(1)}, f32[1,5888]{1,0:T(1,128)S(1)}) custom-call(bf16[384,4096]{1,0:T(8,128)(2,1)} %bitcast.3, bf16[384,1792]{1,0:T(8,128)(2,1)} %bitcast.4, bf16[1792,4096]{1,0:T(8,128)(2,1)} %w_hbm.1), custom_call_target="tpu_custom_call" | custom-call | tf_op jit(solution)/shard_map/pallas_call | solution.py:397
  57.8 1.8 %shard_map.67 = (bf16[384,1792]{1,0:T(8,128)(2,1)}, f32[112,512]{1,0:T(8,128)}, f32[1,112]{1,0:T(1,128)}, f32[1,256]{1,0:T(1,128)}) custom-call(bf16[384,1792]{1,0:T(8,128)(2,1)S(1)} %get-tuple-element.11.gh, f32[112,512]{1,0:T(8,128)S(1)} %get-tuple-element.12.wg, f32[1,5888]{1,0:T(1,128)S(1)} %get-tuple-element.13.pk), custom_call_target="tpu_custom_call" | custom-call | tf_op jit(solution)/shard_map/pallas_call | solution.py:410

commit v4 on v3

--- a/solution.py
+++ b/solution.py
@@ -19,7 +19,6 @@
 EXTRA = ((0, 32), (32, 32), (64, 48))
 PEAKS = FFS + D
 GH = 256
-SPLIT = 80
 
 
 def kernel(g_hbm, h_hbm, w_hbm, gh_v, wg_ref, pk_out,
@@ -31,7 +30,6 @@
     dp = lax.axis_index("dp")
     z, y, x, c = ctx // 4, ctx % 4, dp // 2, dp % 2
     own, rx1, rx2, rx3 = (own0, own1, own2), (r10, r11, r12), (r20, r21, r22), (r30, r31, r32)
-    heights = (144, 144, 160)
 
     def dev(axis, step):
         zz, yy, xx, cc = z, y, x, c
@@ -59,7 +57,7 @@
 
     barrier = pltpu.get_barrier_semaphore()
     friends = [dev("y", d) for d in (1, 2, 3)] + [dev("z", d) for d in (1, 2, 3)]
-    friends += [dev("x", 1), dev("x", 3), dev("c", 1)]
+    friends += [dev("x", d) for d in (1, 2, 3)] + [dev("c", 1)]
     for f in friends:
         pl.semaphore_signal(barrier, inc=1, device_id=f, device_id_type=MESH)
 
@@ -91,6 +89,7 @@
     lax.fori_loop(0, FFS // 256, h_peaks, 0)
     pl.semaphore_wait(barrier, len(friends))
     peer = dev("c", 1)
+    wcopy(0).start()
     swaps = []
     for i in range(4):
         lg[i].wait()
@@ -109,7 +108,7 @@
             size = 384 if r < 15 else 128
             yield r, slice(0, size), slice(r * 384, r * 384 + size)
 
-    for j in range(FFS // GH):
+    for j in range(1, FFS // GH):
         wcopy(j).start()
     for r, a, b in spread(16):
         stage[r : r + 1, a] = pk[0, :, b]
@@ -226,18 +225,11 @@
     axes = (("z", "y", "x"), ("y", "x", "z"), ("x", "z", "y"))
 
     def piece(ph, p, k, half):
-        if ph == 0:
-            return own[p].at[k, pl.ds(2 * half, 2)]
-        if ph == 1:
-            return own[p].at[0, k, pl.ds(2 * half, 2)]
-        rows = pl.ds(0, SPLIT) if half == 0 else pl.ds(SPLIT, heights[p] - SPLIT)
-        return own[p].at[0, 0, k, rows]
+        ref = own[p].at[k] if ph == 0 else own[p].at[0, k]
+        return ref.at[pl.ds(2 * half, 2)]
 
     def landing(ph, p, m, half):
-        ref = (rx1, rx2, rx3)[ph][p].at[m]
-        if ph == 2:
-            return ref.at[pl.ds(0, SPLIT if half == 0 else heights[p] - SPLIT)]
-        return ref
+        return (rx1, rx2)[ph][p].at[m]
 
     flights = {}
     plan = {
@@ -272,29 +264,15 @@
             total = total + o[...].astype(F32)
         ref[...] = total.astype(BF)
 
-    def add_rows(ph, ref, others):
-        if ph:
-            add_into(ref, others)
-            return
-
-        def step(i, _):
-            add_into(ref.at[i], [o.at[i] for o in others])
-            return 0
-
-        lax.fori_loop(0, 4, step, 0)
-
     def onward(ph, p):
-        order = (("-", 0), ("+", 1), ("-", 1), ("+", 0))
-        for sign, idx in order if ph < 2 else (("+", None), ("-", None)):
+        for sign, idx in (("-", 0), ("+", 1), ("-", 1), ("+", 0)):
             got = arrived(ph, p, "a" + sign)
             _, _, k, half = plan["b" + sign]
-            mine = piece(ph, p, k, half)
-            if ph < 2:
-                add_rows(ph, mine.at[idx], [got.at[idx]])
-                post_part(ph, p, "b" + sign, idx)
-            else:
-                add_into(mine, [got])
-                post(ph, p, "b" + sign)
+            add_into(piece(ph, p, k, half).at[idx], [got.at[idx]])
+            post_part(ph, p, "b" + sign, idx)
+
+    def direct(p, k):
+        return remote(own[p].at[0, 0, k], rx3[p].at[k - 1], (6 + p) * 8 + k, dev(axes[p][2], k))
 
     def settle(ph):
         for k in (2, 1, 3, 0):
@@ -304,15 +282,16 @@
                     refs = [arrived(ph, p, "c-").at[idx], arrived(ph, p, "b+", idx)]
                 else:
                     refs = [arrived(ph, p, "c+").at[idx], arrived(ph, p, "b-", idx)]
-                add_rows(ph, own[p].at[(0,) * (ph + 1) + (k,)], refs)
-                if k == 2:
-                    post(ph + 1, p, "a+"), post(ph + 1, p, "a-")
+                add_into(own[p].at[(0,) * (ph + 1) + (k,)], refs)
+                if ph:
+                    if k:
+                        last[p].append(direct(p, k))
+                elif k == 2:
+                    post(1, p, "a+"), post(1, p, "a-")
                 elif k:
-                    post(ph + 1, p, "c+" if k == 1 else "c-")
-
-    def gather_all(ph, p):
-        refs = {n: arrived(ph, p, n) for n in ("c+", "c-", "b+", "b-")}
-        return (refs["b+"], refs["c-"]), (refs["c+"], refs["b-"])
+                    post(1, p, "c+" if k == 1 else "c-")
+
+    last = ([], [], [])
 
     for k in range(4):
         blocks(2, k, 0, 2)
@@ -336,29 +315,25 @@
     for p in (0, 1):
         blocks(p, 0, 0, 4)
 
-    lax.fori_loop(3, FFS // GH, gh_step, 0)
+    lax.fori_loop(3, 6, gh_step, 0)
 
     for p in (2, 0, 1):
         onward(0, p)
+    lax.fori_loop(6, FFS // GH, gh_step, 0)
     settle(0)
     for p in (2, 0, 1):
         onward(1, p)
     settle(1)
     for p in (2, 0, 1):
-        onward(2, p)
-    for p in (2, 0, 1):
-        pair = gather_all(2, p)
         cols = slice(p * 128, p * 128 + 128)
         lo, size = EXTRA[p]
-        for half in (0, 1):
-            total = piece(2, p, 0, half)[...].astype(F32)
-            for o in pair[half]:
-                total = total + o[...].astype(F32)
-            if half == 0:
-                wg_ref[0:SPLIT, cols] = total
-            else:
-                wg_ref[SPLIT:ROWS, cols] = total[: ROWS - SPLIT]
-                wg_ref[lo : lo + size, 384:512] = total[ROWS - SPLIT :]
+        for e in last[p]:
+            e.wait_recv()
+        total = own[p][0, 0, 0].astype(F32)
+        for d in range(3):
+            total = total + rx3[p][d].astype(F32)
+        wg_ref[:, cols] = total[:ROWS]
+        wg_ref[lo : lo + size, 384:512] = total[ROWS:]
     for s in sends:
         s.wait_send()
 
@@ -390,7 +365,7 @@
     scratch += [vm((4, 4, 4, n, 128), BF) for n in heights]
     scratch += [vm((6, 2, 4, n, 128), BF) for n in heights]
     scratch += [vm((6, 2, n, 128), BF) for n in heights]
-    scratch += [vm((6, SPLIT, 128), BF) for n in heights]
+    scratch += [vm((3, n, 128), BF) for n in heights]
     scratch += [dma((5,)), dma((7,)), dma((72,)), dma((72,)), dma((12,)), dma((12,)), dma((7,)), dma((7,))]
     hbm = pl.BlockSpec(memory_space=pltpu.HBM)
     vmspace = pl.BlockSpec(memory_space=pltpu.VMEM)

time: 59.7 us -> 57.7 us (0.966)
  Pallas kernels: 59 us -> 56.8 us
    pallas_call x1, Pallas kernels: 57.1 us -> 54.9 us  [on_device(): pl.pallas_call(kernel, out_shape=(jax.ShapeDtypeStruct((TOK, FFS), BF), j...]
where the time goes in v4:
time: 57.7 us; the launch traced here: 57.6 us
  Pallas kernels  56.8 us (98%)
  between operations  0.8 us (1%)
    pallas_call x1, Pallas kernels, on_device(): pl.pallas_call(kernel, out_shape=(jax.ShapeDtypeStruct((TOK, FFS), BF), j...  54.9 us
    pallas_call x1, Pallas kernels, on_device(): pl.pallas_call(finish, out_shape=(jax.ShapeDtypeStruct((TOK, FFS), BF), j...  1.82 us

profile of v4, /device:TPU:0, one launch (start us, length us, event | category | flops | bytes accessed | tf_op | source)
XLA Modules:
  0.0 57.6 jit_solution(12819109678866461731)
XLA Ops:
  0.6 54.9 %shard_map.66 = (bf16[384,1792]{1,0:T(8,128)(2,1)S(1)}, f32[112,512]{1,0:T(8,128)S(1)}, f32[1,5888]{1,0:T(1,128)S(1)}) custom-call(bf16[384,4096]{1,0:T(8,128)(2,1)} %bitcast.3, bf16[384,1792]{1,0:T(8,128)(2,1)} %bitcast.4, bf16[1792,4096]{1,0:T(8,128)(2,1)} %w_hbm.1), custom_call_target="tpu_custom_call" | custom-call | tf_op jit(solution)/shard_map/pallas_call | solution.py:372
  55.6 1.8 %shard_map.67 = (bf16[384,1792]{1,0:T(8,128)(2,1)}, f32[112,512]{1,0:T(8,128)}, f32[1,112]{1,0:T(1,128)}, f32[1,256]{1,0:T(1,128)}) custom-call(bf16[384,1792]{1,0:T(8,128)(2,1)S(1)} %get-tuple-element.11.gh, f32[112,512]{1,0:T(8,128)S(1)} %get-tuple-element.12.wg, f32[1,5888]{1,0:T(1,128)S(1)} %get-tuple-element.13.pk), custom_call_target="tpu_custom_call" | custom-call | tf_op jit(solution)/shard_map/pallas_call | solution.py:385

commit v5 on v4

--- a/solution.py
+++ b/solution.py
@@ -18,6 +18,7 @@
 ROWS = 112
 EXTRA = ((0, 32), (32, 32), (64, 48))
 PEAKS = FFS + D
+SENDS = 24
 GH = 256
 
 
@@ -25,7 +26,7 @@
            g_own, h_own, g_peer, w_v, hqt, gq, pk,
            stage, am1, am2, am3, amy, amz, amp,
            own0, own1, own2, r10, r11, r12, r20, r21, r22, r30, r31, r32,
-           lsem, wsem, ssem, rsem, s2, q2, hs, hr):
+           lsem, wsem, ssem, rsem):
     ctx = lax.axis_index("ctx")
     dp = lax.axis_index("dp")
     z, y, x, c = ctx // 4, ctx % 4, dp // 2, dp % 2
@@ -63,16 +64,18 @@
 
     sends = []
 
-    def remote(src, dst, i, to, sems=None):
-        a, b = sems or (ssem, rsem)
+    def remote(src, dst, i, to, base=0):
+        slot = len(sends) % SENDS
+        if len(sends) >= SENDS:
+            sends[-SENDS].wait_send()
         copy = pltpu.make_async_remote_copy(
-            src_ref=src, dst_ref=dst, send_sem=a.at[i], recv_sem=b.at[i],
+            src_ref=src, dst_ref=dst, send_sem=ssem.at[slot], recv_sem=rsem.at[base + i],
             device_id=to, device_id_type=MESH)
         copy.start()
         sends.append(copy)
         return copy
 
-    small = (s2, q2)
+    small = 57
 
     def peak_row(ref, lo, size):
         at = pl.ds(pl.multiple_of(lo, 128), size)
@@ -168,13 +171,13 @@
         hqt[at, 0:TOK] = on_grid(h_own[:, at], pk[0, :, at]).T
         if i:
             prev = pl.ds((i - 1) * 256, 256)
-            hsends.append(remote(hqt.at[prev, 0:TOK], hqt.at[prev, TOK:], i - 1, peer, (hs, hr)))
+            hsends.append(remote(hqt.at[prev, 0:TOK], hqt.at[prev, TOK:], i - 1, peer, 69))
     for j in range(2):
         for q in (2, 3):
             quant_g(0, q, j)
         if j == 0:
             prev = pl.ds(FFS - 256, 256)
-            hsends.append(remote(hqt.at[prev, 0:TOK], hqt.at[prev, TOK:], 6, peer, (hs, hr)))
+            hsends.append(remote(hqt.at[prev, 0:TOK], hqt.at[prev, TOK:], 6, peer, 69))
     for j in range(4):
         quant_g(0, 0, j)
         quant_g(0, 1, j)
@@ -272,7 +275,7 @@
             post_part(ph, p, "b" + sign, idx)
 
     def direct(p, k):
-        return remote(own[p].at[0, 0, k], rx3[p].at[k - 1], (6 + p) * 8 + k, dev(axes[p][2], k))
+        return remote(own[p].at[0, 0, k], rx3[p].at[k - 1], 48 + p * 3 + k - 1, dev(axes[p][2], k))
 
     def settle(ph):
         for k in (2, 1, 3, 0):
@@ -334,21 +337,28 @@
             total = total + rx3[p][d].astype(F32)
         wg_ref[:, cols] = total[:ROWS]
         wg_ref[lo : lo + size, 384:512] = total[ROWS:]
-    for s in sends:
+    for s in sends[-SENDS:]:
         s.wait_send()
 
 
-def finish(gh, wg, pk, gh_out, wg_out, ha_out, ga_out, osem):
-    out = pltpu.make_async_copy(gh, gh_out, osem)
-    out.start()
-    wg_out[...] = wg[...] * np.float32(1.0 / np.sqrt(SEQ * REPLICAS))
+def finish(gh, wg, pk, gh_out, wg_out, ha_out, ga_out, wg_v, ha_v, ga_v, osem):
+    outs = [pltpu.make_async_copy(gh, gh_out, osem.at[0])]
+    outs[0].start()
+    wg_v[...] = wg[...] * np.float32(1.0 / np.sqrt(SEQ * REPLICAS))
+    outs.append(pltpu.make_async_copy(wg_v, wg_out, osem.at[1]))
+    outs[1].start()
     ctx = lax.axis_index("ctx")
+    ga_v[...] = pk[:, pl.ds(pl.multiple_of(FFS + ctx * 256, 256), 256)]
+    outs.append(pltpu.make_async_copy(ga_v, ga_out, osem.at[2]))
+    outs[2].start()
     some = pk[:, 0:ROWS]
     for k in range(1, 16):
         some = jnp.where(ctx == k, pk[:, k * ROWS : (k + 1) * ROWS], some)
-    ha_out[...] = some
-    ga_out[...] = pk[:, pl.ds(pl.multiple_of(FFS + ctx * 256, 256), 256)]
-    out.wait()
+    ha_v[...] = some
+    outs.append(pltpu.make_async_copy(ha_v, ha_out, osem.at[3]))
+    outs[3].start()
+    for out in outs:
+        out.wait()
 
 
 def on_device(grad_out, hidden, down_weight):
@@ -366,7 +376,7 @@
     scratch += [vm((6, 2, 4, n, 128), BF) for n in heights]
     scratch += [vm((6, 2, n, 128), BF) for n in heights]
     scratch += [vm((3, n, 128), BF) for n in heights]
-    scratch += [dma((5,)), dma((7,)), dma((72,)), dma((72,)), dma((12,)), dma((12,)), dma((7,)), dma((7,))]
+    scratch += [dma((5,)), dma((7,)), dma((SENDS,)), dma((76,))]
     hbm = pl.BlockSpec(memory_space=pltpu.HBM)
     vmspace = pl.BlockSpec(memory_space=pltpu.VMEM)
     gh, wg, peaks = pl.pallas_call(
@@ -391,8 +401,8 @@
             jax.ShapeDtypeStruct((1, 256), F32),
         ),
         in_specs=[vmspace, vmspace, vmspace],
-        out_specs=(hbm, vmspace, vmspace, vmspace),
-        scratch_shapes=[dma],
+        out_specs=(hbm,) * 4,
+        scratch_shapes=[vm((ROWS, 512), F32), vm((1, ROWS), F32), vm((1, 256), F32), dma((4,))],
         compiler_params=pltpu.CompilerParams(vmem_limit_bytes=8 * 1024 * 1024),
     )(gh, wg, peaks)
     return (gh[None], wg, ha, ga)

time: 57.7 us -> 56.8 us (0.984)
  Pallas kernels: 56.8 us -> 55.9 us
    pallas_call x1, Pallas kernels: 54.9 us -> 54.1 us  [on_device(): pl.pallas_call(kernel, out_shape=(jax.ShapeDtypeStruct((TOK, FFS), BF), j...]
where the time goes in v5:
time: 56.8 us; the launch traced here: 56.7 us
  Pallas kernels  55.9 us (98%)
  between operations  0.8 us (1%)
    pallas_call x1, Pallas kernels, on_device(): pl.pallas_call(kernel, out_shape=(jax.ShapeDtypeStruct((TOK, FFS), BF), j...  54.1 us
    pallas_call x1, Pallas kernels, on_device(): pl.pallas_call(finish, out_shape=(jax.ShapeDtypeStruct((TOK, FFS), BF), j...  1.77 us

profile of v5, /device:TPU:0, one launch (start us, length us, event | category | flops | bytes accessed | tf_op | source)
XLA Modules:
  0.0 56.7 jit_solution(12567531094883958491)
XLA Ops:
  0.6 54.1 %shard_map.66 = (bf16[384,1792]{1,0:T(8,128)(2,1)S(1)}, f32[112,512]{1,0:T(8,128)S(1)}, f32[1,5888]{1,0:T(1,128)S(1)}) custom-call(bf16[384,4096]{1,0:T(8,128)(2,1)} %bitcast.3, bf16[384,1792]{1,0:T(8,128)(2,1)} %bitcast.4, bf16[1792,4096]{1,0:T(8,128)(2,1)} %w_hbm.1), custom_call_target="tpu_custom_call" | custom-call | tf_op jit(solution)/shard_map/pallas_call | solution.py:382
  54.8 1.8 %shard_map.67 = (bf16[384,1792]{1,0:T(8,128)(2,1)}, f32[112,512]{1,0:T(8,128)}, f32[1,112]{1,0:T(1,128)}, f32[1,256]{1,0:T(1,128)}) custom-call(bf16[384,1792]{1,0:T(8,128)(2,1)S(1)} %get-tuple-element.11.gh, f32[112,512]{1,0:T(8,128)S(1)} %get-tuple-element.12.wg, f32[1,5888]{1,0:T(1,128)S(1)} %get-tuple-element.13.pk), custom_call_target="tpu_custom_call" | custom-call | tf_op jit(solution)/shard_map/pallas_call | solution.py:395

commit v6 on v5

--- a/solution.py
+++ b/solution.py
@@ -18,7 +18,7 @@
 ROWS = 112
 EXTRA = ((0, 32), (32, 32), (64, 48))
 PEAKS = FFS + D
-SENDS = 24
+SENDS = 22
 GH = 256
 
 
@@ -75,7 +75,7 @@
         sends.append(copy)
         return copy
 
-    small = 57
+    small = 56
 
     def peak_row(ref, lo, size):
         at = pl.ds(pl.multiple_of(lo, 128), size)
@@ -169,15 +169,15 @@
     for i in range(FFS // 256):
         at = pl.ds(i * 256, 256)
         hqt[at, 0:TOK] = on_grid(h_own[:, at], pk[0, :, at]).T
-        if i:
-            prev = pl.ds((i - 1) * 256, 256)
-            hsends.append(remote(hqt.at[prev, 0:TOK], hqt.at[prev, TOK:], i - 1, peer, 69))
+        if i in (2, 4, 6):
+            prev = pl.ds((i - 2) * 256, 512)
+            hsends.append(remote(hqt.at[prev, 0:TOK], hqt.at[prev, TOK:], i // 2 - 1, peer, 68))
     for j in range(2):
         for q in (2, 3):
             quant_g(0, q, j)
         if j == 0:
             prev = pl.ds(FFS - 256, 256)
-            hsends.append(remote(hqt.at[prev, 0:TOK], hqt.at[prev, TOK:], 6, peer, 69))
+            hsends.append(remote(hqt.at[prev, 0:TOK], hqt.at[prev, TOK:], 3, peer, 68))
     for j in range(4):
         quant_g(0, 0, j)
         quant_g(0, 1, j)
@@ -376,7 +376,7 @@
     scratch += [vm((6, 2, 4, n, 128), BF) for n in heights]
     scratch += [vm((6, 2, n, 128), BF) for n in heights]
     scratch += [vm((3, n, 128), BF) for n in heights]
-    scratch += [dma((5,)), dma((7,)), dma((SENDS,)), dma((76,))]
+    scratch += [dma((5,)), dma((7,)), dma((SENDS,)), dma((72,))]
     hbm = pl.BlockSpec(memory_space=pltpu.HBM)
     vmspace = pl.BlockSpec(memory_space=pltpu.VMEM)
     gh, wg, peaks = pl.pallas_call(

time: 56.8 us -> 55.9 us (0.984)
  Pallas kernels: 55.9 us -> 55 us
    pallas_call x1, Pallas kernels: 54.1 us -> 53.2 us  [on_device(): pl.pallas_call(kernel, out_shape=(jax.ShapeDtypeStruct((TOK, FFS), BF), j...]
where the time goes in v6:
time: 55.9 us; the launch traced here: 55.8 us
  Pallas kernels  55 us (98%)
  between operations  0.8 us (1%)
    pallas_call x1, Pallas kernels, on_device(): pl.pallas_call(kernel, out_shape=(jax.ShapeDtypeStruct((TOK, FFS), BF), j...  53.2 us
    pallas_call x1, Pallas kernels, on_device(): pl.pallas_call(finish, out_shape=(jax.ShapeDtypeStruct((TOK, FFS), BF), j...  1.77 us

profile of v6, /device:TPU:0, one launch (start us, length us, event | category | flops | bytes accessed | tf_op | source)
XLA Modules:
  0.0 55.8 jit_solution(89281353206371299)
XLA Ops:
  0.6 53.2 %shard_map.66 = (bf16[384,1792]{1,0:T(8,128)(2,1)S(1)}, f32[112,512]{1,0:T(8,128)S(1)}, f32[1,5888]{1,0:T(1,128)S(1)}) custom-call(bf16[384,4096]{1,0:T(8,128)(2,1)} %bitcast.3, bf16[384,1792]{1,0:T(8,128)(2,1)} %bitcast.4, bf16[1792,4096]{1,0:T(8,128)(2,1)} %w_hbm.1), custom_call_target="tpu_custom_call" | custom-call | tf_op jit(solution)/shard_map/pallas_call | solution.py:382
  53.9 1.8 %shard_map.67 = (bf16[384,1792]{1,0:T(8,128)(2,1)}, f32[112,512]{1,0:T(8,128)}, f32[1,112]{1,0:T(1,128)}, f32[1,256]{1,0:T(1,128)}) custom-call(bf16[384,1792]{1,0:T(8,128)(2,1)S(1)} %get-tuple-element.11.gh, f32[112,512]{1,0:T(8,128)S(1)} %get-tuple-element.12.wg, f32[1,5888]{1,0:T(1,128)S(1)} %get-tuple-element.13.pk), custom_call_target="tpu_custom_call" | custom-call | tf_op jit(solution)/shard_map/pallas_call | solution.py:395
